TPU v7x, 32 devices: a whole 2x2x4 slice. The times are simulated.
32 devices in a mesh: rows: 16 (over z, y, x), sub: 2 (over core).
Axes of the slice: x: 2, y: 2, z: 4, core: 2. Of those that a mesh axis runs over, the one named last changes fastest.
Arguments:
- matrix: float32 [4096, 384], P(('rows', 'sub')), as said below
- grad_out: float32 [4096, 384], P(('rows', 'sub')), as said below
- grad_factor: float32 [384, 384], replicated, may hold values from -6 to 6
Outputs:
- grad_matrix: float32 [4096, 384], P(('rows', 'sub'))
Inputs may be any that keep to these rules, and one draw needn't show every extreme that they name: `matrix`: entries at most of order 1 / sqrt(4096), with a scale that varies by row and by column. `grad_out`: entries of order 0.01.
All inputs are finite; a program needn't handle non-finite values.
Results may differ from a plain program's by a relative error of at most 0.0004.
Values sent between devices are 32-bit elements; how exact they have to be, the bound alone decides.
No kernel may reach another device: no remote copies, remote signals or barrier semaphores. Data moves between devices by JAX's collectives and lax.ppermute only.
A program may use at most 64 MiB of HBM per device.

v0:
```python
import jax
import jax.numpy as jnp
from jax import lax
from jax.sharding import PartitionSpec as P

SECTIONS = 2
shift_frac = 0.02


def full_dot(left, right):
    return jnp.dot(left, right, precision=lax.Precision.HIGHEST, preferred_element_type=jnp.float32)


def inner_gram(left, right):
    return lax.dot_general(
        left,
        right,
        (((0,), (0,)), ((), ())),
        precision=lax.Precision.HIGHEST,
        preferred_element_type=jnp.float32,
    )


def cholesky_adjoint(lower_fac, lower_inv, lower_grad):
    product = full_dot(lower_fac.T, lower_grad)
    phi_part = jnp.tril(product) - 0.5 * jnp.diag(jnp.diag(product))
    sandwich = full_dot(full_dot(lower_inv.T, phi_part), lower_inv)
    return 0.5 * (sandwich + sandwich.T)


def factor_grads(uppers, grad_factor):
    count = len(uppers)
    result = []
    for section_index in range(count):
        middle = grad_factor
        for later in range(section_index + 1, count):
            middle = full_dot(uppers[later].T, middle)
        for earlier in range(section_index - 1, -1, -1):
            middle = full_dot(middle, uppers[earlier].T)
        result.append(middle)
    return result


def summed_gram(partial_value):
    half_rows = lax.psum_scatter(partial_value, "sub", scatter_dimension=0, tiled=True)
    half_rows = lax.psum(half_rows, "rows")
    return lax.all_gather(half_rows, "sub", axis=0, tiled=True)


def per_device(matrix, grad_out, grad_factor):
    width = matrix.shape[1]
    rate = shift_frac / width
    identity = jnp.eye(width, dtype=jnp.float32)
    current = matrix
    saved = []
    for section_index in range(SECTIONS):
        summed = summed_gram(inner_gram(current, current))
        shift_val = rate * jnp.trace(summed)
        lower_fac = jnp.linalg.cholesky(summed + shift_val * identity)
        lower_inv = lax.linalg.triangular_solve(lower_fac, identity, left_side=True, lower=True)
        following = full_dot(current, lower_inv.T)
        saved.append((current, following, lower_fac, lower_inv))
        current = following
    uppers = [item[2].T for item in saved]
    fac_grads = factor_grads(uppers, grad_factor)
    q_grad = grad_out
    for section_index in range(SECTIONS - 1, -1, -1):
        before, after, lower_fac, lower_inv = saved[section_index]
        crossed = lax.psum(inner_gram(after, q_grad), ("rows", "sub"))
        total_grad = fac_grads[section_index] - full_dot(crossed, lower_inv)
        gram_grad = cholesky_adjoint(lower_fac, lower_inv, jnp.tril(total_grad.T))
        gram_grad = gram_grad + rate * jnp.trace(gram_grad) * identity
        q_grad = full_dot(q_grad, lower_inv) + 2.0 * full_dot(before, gram_grad)
    return q_grad


def solution(mesh):
    placed = (P(("rows", "sub"), None), P(("rows", "sub"), None), P())
    return jax.shard_map(
        per_device, mesh=mesh, in_specs=placed, out_specs=P(("rows", "sub"), None), check_vma=False
    )
```

profile of v0, /device:TPU:0, one launch (start us, length us, event | category | flops | bytes accessed | tf_op | source)
XLA Modules:
  0.0 777.9 jit_solution(7228258176599560391)
XLA Ops:
  6.5 2.6 fusion.120
  9.2 11.2 %reduce-scatter.7.cloned.1.call-done = f32[192,384]{1,0:T(8,128)} async-done(((f32[384,384]{1,0:T(8,128)}), f32[192,384]{1,0:T(8,128)}) %reduce-scatter.7.cloned.1.call-update) | async-done | bytes 294928
  20.3 1.9 copy.59
  22.4 113.0 %all-reduce.6.cloned.1.call-done = f32[192,384]{0,1:T(8,128)} async-done(((f32[192,384]{0,1:T(8,128)}), f32[192,384]{0,1:T(8,128)}) %all-reduce.6.cloned.1.call-update) | async-done | bytes 294928 | tf_op jit(solution)/shard_map/psum | solution.py:46
  135.3 1.1 copy.25
  136.5 2.2 all_gather.6
  140.5 11.7 %cholesky.208 = f32[128,128]{1,0:T(8,128)S(1)} custom-call(f32[128,128]{1,0:T(8,128)S(1)} %cholesky.310), custom_call_target="Cholesky" | custom-call | tf_op jit(solution)/shard_map/jit(cholesky)/cholesky | solution.py:59
  152.3 9.8 %custom-call.24 = f32[1,128,128]{1,2,0:T(8,128)S(1)} custom-call(f32[1,128,128]{2,1,0:T(8,128)S(1)} %get-tuple-element.56), custom_call_target="InvertDiagBlocksLowerTriangular" | custom-call | tf_op jit(solution)/shard_map/jit(cholesky)/cholesky | solution.py:59
  162.7 11.7 %cholesky.227 = f32[128,128]{1,0:T(8,128)S(1)} custom-call(f32[128,128]{1,0:T(8,128)S(1)} %cholesky.314), custom_call_target="Cholesky" | custom-call | tf_op jit(solution)/shard_map/jit(cholesky)/cholesky | solution.py:59
  174.5 10.0 %custom-call.25 = f32[1,128,128]{1,2,0:T(8,128)S(1)} custom-call(f32[1,128,128]{2,1,0:T(8,128)S(1)} %get-tuple-element.53), custom_call_target="InvertDiagBlocksLowerTriangular" | custom-call | tf_op jit(solution)/shard_map/jit(cholesky)/cholesky | solution.py:59
  184.9 11.7 %cholesky.246 = f32[128,128]{1,0:T(8,128)S(1)} custom-call(f32[128,128]{1,0:T(8,128)S(1)} %convolution_subtract_fusion.9), custom_call_target="Cholesky" | custom-call | tf_op jit(solution)/shard_map/jit(cholesky)/cholesky | solution.py:59
  200.0 6.0 while.4
  200.7 1.3 bitcast_dynamic-update-slice_fusion.4
  202.7 1.3 bitcast_dynamic-update-slice_fusion.4
  204.7 1.3 bitcast_dynamic-update-slice_fusion.4
  206.0 29.5 %custom-call.26 = f32[3,128,128]{1,2,0:T(8,128)S(1)} custom-call(f32[3,128,128]{2,1,0:T(8,128)S(1)} %get-tuple-element.21), custom_call_target="InvertDiagBlocksLowerTriangular" | custom-call | tf_op jit(solution)/shard_map/triangular_solve/custom-call.2 | solution.py:60
  236.8 0.8 convolution_subtract_fusion.4
  239.2 1.4 fusion.121
  240.7 7.1 reduce-scatter.9.cloned.1.call-done
  247.8 1.9 copy.61
  249.8 112.9 %all-reduce.8.cloned.1.call-done = f32[192,384]{0,1:T(8,128)} async-done(((f32[192,384]{0,1:T(8,128)}), f32[192,384]{0,1:T(8,128)}) %all-reduce.8.cloned.1.call-update) | async-done | bytes 294928 | tf_op jit(solution)/shard_map/psum | solution.py:46
  362.7 1.1 copy.32
  363.8 2.4 all_gather.7
  367.8 1.0 copy.35
  368.8 1.1 fusion.6
  370.0 11.7 %cholesky.261 = f32[128,128]{1,0:T(8,128)S(1)} custom-call(f32[128,128]{1,0:T(8,128)S(1)} %cholesky.318), custom_call_target="Cholesky" | custom-call | tf_op jit(solution)/shard_map/jit(cholesky)/cholesky | solution.py:59
  381.8 9.8 %custom-call.27 = f32[1,128,128]{1,2,0:T(8,128)S(1)} custom-call(f32[1,128,128]{2,1,0:T(8,128)S(1)} %get-tuple-element.49), custom_call_target="InvertDiagBlocksLowerTriangular" | custom-call | tf_op jit(solution)/shard_map/jit(cholesky)/cholesky | solution.py:59
  392.2 11.7 %cholesky.280 = f32[128,128]{1,0:T(8,128)S(1)} custom-call(f32[128,128]{1,0:T(8,128)S(1)} %cholesky.322), custom_call_target="Cholesky" | custom-call | tf_op jit(solution)/shard_map/jit(cholesky)/cholesky | solution.py:59
  405.3 10.2 %custom-call.28 = f32[1,128,128]{1,2,0:T(8,128)S(1)} custom-call(f32[1,128,128]{2,1,0:T(8,128)S(1)} %get-tuple-element.46), custom_call_target="InvertDiagBlocksLowerTriangular" | custom-call | tf_op jit(solution)/shard_map/jit(cholesky)/cholesky | solution.py:59
  416.0 11.7 %cholesky.299 = f32[128,128]{1,0:T(8,128)S(1)} custom-call(f32[128,128]{1,0:T(8,128)S(1)} %convolution_subtract_fusion.8), custom_call_target="Cholesky" | custom-call | tf_op jit(solution)/shard_map/jit(cholesky)/cholesky | solution.py:59
  430.4 0.9 fusion.11
  431.3 8.7 %while.5 = (s32[]{:T(128)}, f32[384,384]{1,0:T(8,128)}, s32[3,2]{0,1:T(2,128)S(1)}, f32[3,128,128]{2,1,0:T(8,128)S(1)}, s32[]{:T(128)}) while((s32[]{:T(128)}, f32[384,384]{1,0:T(8,128)}, s32[3,2]{0,1:T(2,128)S(1)}, f32[3,128,128]{2,1,0:T(8,128)S(1)}, s32[]{:T(128)}) %tuple.65), condition=%wide.while_cond.clone, body=%wide.while_body.clone.sunk | while | flops 2 | bytes 131181 | solution.py:60
  431.9 2.2 bitcast_dynamic-update-slice_fusion.5
  434.8 2.2 bitcast_dynamic-update-slice_fusion.5
  437.8 2.2 bitcast_dynamic-update-slice_fusion.5
  439.9 29.5 %custom-call.29 = f32[3,128,128]{1,2,0:T(8,128)S(1)} custom-call(f32[3,128,128]{2,1,0:T(8,128)S(1)} %get-tuple-element.22), custom_call_target="InvertDiagBlocksLowerTriangular" | custom-call | tf_op jit(solution)/shard_map/triangular_solve/custom-call.2 | solution.py:60
  470.1 1.3 convolution_subtract_fusion.3
  471.5 1.2 fusion.78
  472.7 1.7 convolution_subtract_fusion.2
  474.4 1.2 fusion.76
  475.7 0.8 fusion.115
  476.7 1.5 fusion.122
  478.5 2.1 fusion.38
  480.6 125.3 %all-reduce.10.cloned.1.call-done = f32[384,384]{1,0:T(8,128)} async-done(((f32[384,384]{1,0:T(8,128)}), f32[384,384]{1,0:T(8,128)}) %all-reduce.10.cloned.1.call-update) | async-done | bytes 589840 | tf_op jit(solution)/shard_map/psum | solution.py:69
  605.9 2.5 fusion
  608.4 1.5 fusion.34
  609.9 1.0 copy.40
  611.0 3.4 gather_fusion
  614.4 3.3 fusion.21
  617.7 1.3 fusion.114
  619.0 1.0 copy.41
  620.0 1.7 select_reduce_fusion.1
  622.4 1.8 convolution_multiply_fusion.1
  624.2 1.1 fusion.3
  625.3 1.4 fusion.123
  626.8 1.3 convolution_bitcast_fusion
  628.1 127.6 %all-reduce.12.cloned.1.call-done = f32[384,384]{1,0:T(8,128)} async-done(((f32[384,384]{1,0:T(8,128)}), f32[384,384]{1,0:T(8,128)}) %all-reduce.12.cloned.1.call-update) | async-done | bytes 589840 | tf_op jit(solution)/shard_map/psum | solution.py:69
  755.7 2.4 fusion.1
  758.1 1.5 fusion.36
  759.8 3.7 gather_fusion.1
  763.5 2.1 fusion.14
  765.6 1.3 fusion.116
  768.6 0.8 fusion.2
  769.5 1.3 convolution_add_fusion
  (103 shorter events, 17.5 us)
Async XLA Ops:
  6.5 471.9 %copy-start = (f32[384,384]{1,0:T(8,128)S(1)}, f32[384,384]{1,0:T(8,128)}, u32[]{:S(2)}) copy-start(f32[384,384]{1,0:T(8,128)} %param.8) | copy-start | bytes 1769476
  6.5 13.8 %reduce-scatter.7.cloned.1.call-start = ((), (), s32[]{:S(2)}) async-start(), calls=%async_computation.6 | async-start | bytes 884736
  9.1 126.2 %all-reduce.6.cloned.1.call-start = ((), (), s32[]{:S(2)}) async-start(), calls=%async_computation.2 | async-start | bytes 786432 | tf_op jit(solution)/shard_map/psum | solution.py:46
  22.2 225.6 %reduce-scatter.9.cloned.1.call-start = ((), (), s32[]{:S(2)}) async-start(), calls=%async_computation.7 | async-start | bytes 884736
  22.3 214.5 %copy-start.1 = (f32[384,384]{0,1:T(8,128)}, f32[384,384]{0,1:T(8,128)S(1)}, u32[]{:S(2)}) copy-start(f32[384,384]{0,1:T(8,128)S(1)} %fusion.26) | copy-start | bytes 1769476
  237.6 0.9 copy-start.6
  240.7 122.0 %all-reduce.8.cloned.1.call-start = ((), (), s32[]{:S(2)}) async-start(), calls=%async_computation.3 | async-start | bytes 786432 | tf_op jit(solution)/shard_map/psum | solution.py:46
  249.7 356.1 %all-reduce.10.cloned.1.call-start = ((), (), s32[]{:S(2)}) async-start(), calls=%async_computation.4 | async-start | bytes 1179648 | tf_op jit(solution)/shard_map/psum | solution.py:69
  370.0 11.7 %copy-start.10 = (f32[384,384]{1,0:T(8,128)}, f32[384,384]{1,0:T(8,128)S(1)}, u32[]{:S(2)}) copy-start(f32[384,384]{1,0:T(8,128)S(1)} %fusion.6) | copy-start | bytes 1769476
  381.7 9.9 %copy-start.11 = (f32[384,384]{1,0:T(8,128)S(1)}, f32[384,384]{1,0:T(8,128)}, u32[]{:S(2)}) copy-start(f32[384,384]{1,0:T(8,128)} %copy-done.10) | copy-start | bytes 1769476
  430.4 39.1 %copy-start.2 = (f32[384,384]{0,1:T(8,128)S(1)}, f32[384,384]{0,1:T(8,128)}, u32[]{:S(2)}) copy-start(f32[384,384]{0,1:T(8,128)} %copy-done.1) | copy-start | bytes 1769476
  469.5 0.7 copy-start.14
  475.7 130.2 %copy-start.3 = (f32[128,384]{1,0:T(8,128)}, f32[128,384]{1,0:T(8,128)S(1)}, u32[]{:S(2)}) copy-start(f32[128,384]{1,0:T(8,128)S(1)} %fusion.76) | copy-start | bytes 589828
  475.7 1.0 copy-start.12
  478.2 277.5 %all-reduce.12.cloned.1.call-start = ((), (), s32[]{:S(2)}) async-start(), calls=%async_computation.5 | async-start | bytes 1179648 | tf_op jit(solution)/shard_map/psum | solution.py:69
  614.4 3.3 copy-start.4
  622.3 1.8 copy-start.5
  622.3 1.8 copy-start.13
  625.3 1.5 copy-start.8
  767.1 1.4 copy-start.7
  768.5 0.9 copy-start.9
Sparse Core Ops, SparseCore 0:
  9.6 10.6 reduce-scatter.6
  25.5 109.7 all-reduce.5
  240.8 6.9 reduce-scatter.8
  252.9 109.7 all-reduce.7
  478.4 127.4 all-reduce.9
  626.9 128.7 all-reduce.11
where the time goes:
time: 788 us; the launch traced here: 778 us
  waiting for transfers between devices  497 us (63%)
  other arithmetic  179 us (23%)
  matrix products  43.1 us (5%)
  local copies, waits for them, and re-layouts  33.2 us (4%)
  between operations  20.5 us (3%)
    psum x2, waiting for transfers between devices, per_device(): crossed = lax.psum(inner_gram(after, q_grad), ('rows', 'sub'))  253 us
    psum x2, waiting for transfers between devices, summed_gram(): half_rows = lax.psum(half_rows, 'rows')  226 us
    another operation x21, other arithmetic, per_device(): lower_fac = jnp.linalg.cholesky(summed + shift_val * identity)  114 us
    another operation x5, other arithmetic, per_device(): lax.linalg.triangular_solve(lower_fac, identity, left_side=True, lower=True)  59.9 us
    dot_general x16, matrix products, full_dot(): jnp.dot(left, right, precision=lax.Precision.HIGHEST, preferred_element_t...  25.7 us
    unnamed x8, waiting for transfers between devices  18.4 us
  transfers between devices with their start and end apart: 6, of which 6 were waited for; matrix products, arithmetic and copies ran while one was open for 0% of the time, Pallas kernels for 0%

commit v1 on v0

--- a/solution.py
+++ b/solution.py
@@ -43,7 +43,7 @@
 
 def summed_gram(partial_value):
     half_rows = lax.psum_scatter(partial_value, "sub", scatter_dimension=0, tiled=True)
-    half_rows = lax.psum(half_rows, "rows")
+    half_rows = jnp.sum(lax.all_gather(half_rows, "rows"), axis=0)
     return lax.all_gather(half_rows, "sub", axis=0, tiled=True)
 
 

time: 788 us -> 740 us (0.939)
  waiting for transfers between devices: 497 us -> 438 us
  matrix products: 43.1 us -> 51.1 us
    psum x2 -> x0, waiting for transfers between devices: 226 us -> none  [summed_gram(): half_rows = lax.psum(half_rows, 'rows')]
    all_gather x0 -> x2, waiting for transfers between devices: none -> 167 us  [summed_gram(): half_rows = jnp.sum(lax.all_gather(half_rows, 'rows'), axis=0)]
    unnamed x8 -> x6, waiting for transfers between devices: 18.4 us -> 0.1 us
    reduce_scatter x0 -> x2, waiting for transfers between devices: none -> 17.9 us  [summed_gram(): lax.psum_scatter(partial_value, 'sub', scatter_dimension=0, tiled=True)]
where the time goes in v1:
time: 740 us; the launch traced here: 729 us
  waiting for transfers between devices  438 us (59%)
  other arithmetic  185 us (25%)
  matrix products  51.1 us (7%)
  local copies, waits for them, and re-layouts  30.2 us (4%)
  between operations  20.6 us (3%)
    psum x2, waiting for transfers between devices, per_device(): crossed = lax.psum(inner_gram(after, q_grad), ('rows', 'sub'))  253 us
    all_gather x2, waiting for transfers between devices, summed_gram(): half_rows = jnp.sum(lax.all_gather(half_rows, 'rows'), axis=0)  167 us
    another operation x21, other arithmetic, per_device(): lower_fac = jnp.linalg.cholesky(summed + shift_val * identity)  114 us
    another operation x5, other arithmetic, per_device(): lax.linalg.triangular_solve(lower_fac, identity, left_side=True, lower=True)  59.9 us
    dot_general x16, matrix products, full_dot(): jnp.dot(left, right, precision=lax.Precision.HIGHEST, preferred_element_t...  27.4 us
    reduce_scatter x2, waiting for transfers between devices, summed_gram(): lax.psum_scatter(partial_value, 'sub', scatter_dimension=0, tiled=True)  17.9 us
  transfers between devices with their start and end apart: 6, of which 6 were waited for; matrix products, arithmetic and copies ran while one was open for 0% of the time, Pallas kernels for 0%

profile of v1, /device:TPU:0, one launch (start us, length us, event | category | flops | bytes accessed | tf_op | source)
XLA Modules:
  0.0 729.5 jit_solution(6322254099449447524)
XLA Ops:
  6.5 2.6 fusion.120
  9.2 11.2 %reduce-scatter.3.cloned.1.call-done = f32[192,384]{1,0:T(8,128)} async-done(((f32[384,384]{1,0:T(8,128)}), f32[192,384]{1,0:T(8,128)}) %reduce-scatter.3.cloned.1.call-update) | async-done | bytes 294928 | tf_op jit(solution)/shard_map/reduce_scatter | solution.py:45
  20.5 83.5 %all-gather.5.cloned.1.call-done = f32[3072,384]{1,0:T(8,128)} async-done(((f32[192,384]{1,0:T(8,128)}), f32[3072,384]{1,0:T(8,128)}) %all-gather.5.cloned.1.call-update) | async-done | bytes 4718608 | tf_op jit(solution)/shard_map/all_gather | solution.py:46
  104.0 2.6 reduce_sum.37
  106.6 2.2 all_gather.20
  111.6 11.7 %cholesky.208 = f32[128,128]{1,0:T(8,128)S(1)} custom-call(f32[128,128]{1,0:T(8,128)S(1)} %cholesky.310), custom_call_target="Cholesky" | custom-call | tf_op jit(solution)/shard_map/jit(cholesky)/cholesky | solution.py:59
  123.4 9.8 %custom-call.24 = f32[1,128,128]{1,2,0:T(8,128)S(1)} custom-call(f32[1,128,128]{2,1,0:T(8,128)S(1)} %get-tuple-element.56), custom_call_target="InvertDiagBlocksLowerTriangular" | custom-call | tf_op jit(solution)/shard_map/jit(cholesky)/cholesky | solution.py:59
  133.3 1.2 constant_dynamic-update-slice_fusion.3
  134.4 1.2 convolution_subtract_fusion.7
  135.6 11.7 %cholesky.227 = f32[128,128]{1,0:T(8,128)S(1)} custom-call(f32[128,128]{1,0:T(8,128)S(1)} %cholesky.314), custom_call_target="Cholesky" | custom-call | tf_op jit(solution)/shard_map/jit(cholesky)/cholesky | solution.py:59
  147.4 10.0 %custom-call.25 = f32[1,128,128]{1,2,0:T(8,128)S(1)} custom-call(f32[1,128,128]{2,1,0:T(8,128)S(1)} %get-tuple-element.53), custom_call_target="InvertDiagBlocksLowerTriangular" | custom-call | tf_op jit(solution)/shard_map/jit(cholesky)/cholesky | solution.py:59
  157.6 1.1 convolution_subtract_fusion.9
  158.7 11.7 %cholesky.246 = f32[128,128]{1,0:T(8,128)S(1)} custom-call(f32[128,128]{1,0:T(8,128)S(1)} %convolution_subtract_fusion.9), custom_call_target="Cholesky" | custom-call | tf_op jit(solution)/shard_map/jit(cholesky)/cholesky | solution.py:59
  173.8 6.1 while.4
  174.5 1.3 bitcast_dynamic-update-slice_fusion.4
  176.5 1.3 bitcast_dynamic-update-slice_fusion.4
  178.6 1.3 bitcast_dynamic-update-slice_fusion.4
  179.9 29.5 %custom-call.26 = f32[3,128,128]{1,2,0:T(8,128)S(1)} custom-call(f32[3,128,128]{2,1,0:T(8,128)S(1)} %get-tuple-element.21), custom_call_target="InvertDiagBlocksLowerTriangular" | custom-call | tf_op jit(solution)/shard_map/triangular_solve/custom-call.2 | solution.py:60
  212.6 1.4 fusion.121
  214.1 6.8 reduce-scatter.5.cloned.1.call-done
  220.9 83.4 %all-gather.7.cloned.1.call-done = f32[3072,384]{1,0:T(8,128)} async-done(((f32[192,384]{1,0:T(8,128)}), f32[3072,384]{1,0:T(8,128)}) %all-gather.7.cloned.1.call-update) | async-done | bytes 4718608 | tf_op jit(solution)/shard_map/all_gather | solution.py:46
  304.4 2.6 reduce_sum.48
  306.9 2.6 all_gather.23
  309.5 1.3 copy.26
  313.1 2.1 copy.27
  315.2 1.1 fusion.6
  317.2 11.7 %cholesky.261 = f32[128,128]{1,0:T(8,128)S(1)} custom-call(f32[128,128]{1,0:T(8,128)S(1)} %cholesky.318), custom_call_target="Cholesky" | custom-call | tf_op jit(solution)/shard_map/jit(cholesky)/cholesky | solution.py:59
  329.0 9.8 %custom-call.27 = f32[1,128,128]{1,2,0:T(8,128)S(1)} custom-call(f32[1,128,128]{2,1,0:T(8,128)S(1)} %get-tuple-element.49), custom_call_target="InvertDiagBlocksLowerTriangular" | custom-call | tf_op jit(solution)/shard_map/jit(cholesky)/cholesky | solution.py:59
  338.8 1.2 constant_dynamic-update-slice_fusion.1
  339.9 1.2 convolution_subtract_fusion.6
  341.1 11.7 %cholesky.280 = f32[128,128]{1,0:T(8,128)S(1)} custom-call(f32[128,128]{1,0:T(8,128)S(1)} %cholesky.322), custom_call_target="Cholesky" | custom-call | tf_op jit(solution)/shard_map/jit(cholesky)/cholesky | solution.py:59
  354.2 10.2 %custom-call.28 = f32[1,128,128]{1,2,0:T(8,128)S(1)} custom-call(f32[1,128,128]{2,1,0:T(8,128)S(1)} %get-tuple-element.46), custom_call_target="InvertDiagBlocksLowerTriangular" | custom-call | tf_op jit(solution)/shard_map/jit(cholesky)/cholesky | solution.py:59
  364.7 1.1 convolution_subtract_fusion.8
  365.8 11.7 %cholesky.299 = f32[128,128]{1,0:T(8,128)S(1)} custom-call(f32[128,128]{1,0:T(8,128)S(1)} %convolution_subtract_fusion.8), custom_call_target="Cholesky" | custom-call | tf_op jit(solution)/shard_map/jit(cholesky)/cholesky | solution.py:59
  381.1 8.6 %while.5 = (s32[]{:T(128)}, f32[384,384]{1,0:T(8,128)}, s32[3,2]{0,1:T(2,128)S(1)}, f32[3,128,128]{2,1,0:T(8,128)S(1)}, s32[]{:T(128)}) while((s32[]{:T(128)}, f32[384,384]{1,0:T(8,128)}, s32[3,2]{0,1:T(2,128)S(1)}, f32[3,128,128]{2,1,0:T(8,128)S(1)}, s32[]{:T(128)}) %tuple.65), condition=%wide.while_cond.clone, body=%wide.while_body.clone.sunk | while | flops 2 | bytes 131181 | solution.py:60
  381.7 2.2 bitcast_dynamic-update-slice_fusion.5
  384.6 2.2 bitcast_dynamic-update-slice_fusion.5
  387.5 2.2 bitcast_dynamic-update-slice_fusion.5
  389.7 29.5 %custom-call.29 = f32[3,128,128]{1,2,0:T(8,128)S(1)} custom-call(f32[3,128,128]{2,1,0:T(8,128)S(1)} %get-tuple-element.22), custom_call_target="InvertDiagBlocksLowerTriangular" | custom-call | tf_op jit(solution)/shard_map/triangular_solve/custom-call.2 | solution.py:60
  419.9 1.3 convolution_subtract_fusion.3
  421.2 1.2 fusion.78
  422.5 1.7 convolution_subtract_fusion.2
  424.2 1.2 fusion.76
  426.3 2.5 fusion.122
  429.0 2.1 fusion.38
  431.1 125.0 %all-reduce.4.cloned.1.call-done = f32[384,384]{1,0:T(8,128)} async-done(((f32[384,384]{1,0:T(8,128)}), f32[384,384]{1,0:T(8,128)}) %all-reduce.4.cloned.1.call-update) | async-done | bytes 589840 | tf_op jit(solution)/shard_map/psum | solution.py:69
  556.0 2.5 fusion
  558.6 1.5 fusion.34
  560.1 1.0 copy.32
  561.1 3.4 gather_fusion
  564.5 3.3 fusion.21
  567.8 2.2 fusion.114
  571.1 1.7 select_reduce_fusion.1
  573.3 1.8 convolution_multiply_fusion.1
  575.1 2.2 fusion.3
  577.3 1.4 fusion.123
  578.7 1.3 convolution_bitcast_fusion
  580.0 127.6 %all-reduce.6.cloned.1.call-done = f32[384,384]{1,0:T(8,128)} async-done(((f32[384,384]{1,0:T(8,128)}), f32[384,384]{1,0:T(8,128)}) %all-reduce.6.cloned.1.call-update) | async-done | bytes 589840 | tf_op jit(solution)/shard_map/psum | solution.py:69
  707.6 2.4 fusion.1
  710.0 1.5 fusion.36
  711.7 3.7 gather_fusion.1
  715.4 2.1 fusion.14
  717.5 1.3 fusion.116
  721.1 1.3 convolution_add_fusion
  (85 shorter events, 21.7 us)
Async XLA Ops:
  6.5 422.5 %copy-start = (f32[384,384]{1,0:T(8,128)S(1)}, f32[384,384]{1,0:T(8,128)}, u32[]{:S(2)}) copy-start(f32[384,384]{1,0:T(8,128)} %param.8) | copy-start | bytes 1769476
  6.5 13.8 %reduce-scatter.3.cloned.1.call-start = ((), (), s32[]{:S(2)}) async-start(), calls=%async_computation.2 | async-start | bytes 884736 | tf_op jit(solution)/shard_map/reduce_scatter | solution.py:45
  9.1 94.9 %all-gather.5.cloned.1.call-start = ((), (), s32[]{:S(2)}) async-start(), calls=%async_computation.6 | async-start | bytes 5013504 | tf_op jit(solution)/shard_map/all_gather | solution.py:46
  20.4 200.5 %reduce-scatter.5.cloned.1.call-start = ((), (), s32[]{:S(2)}) async-start(), calls=%async_computation.3 | async-start | bytes 884736 | tf_op jit(solution)/shard_map/reduce_scatter | solution.py:45
  110.7 101.2 %copy-start.2 = (f32[128,384]{1,0:T(8,128)S(1)}, f32[128,384]{1,0:T(8,128)}, u32[]{:S(2)}) copy-start(f32[128,384]{1,0:T(8,128)} %param.6) | copy-start | bytes 589828
  110.8 0.8 copy-start.5
  214.1 90.3 %all-gather.7.cloned.1.call-start = ((), (), s32[]{:S(2)}) async-start(), calls=%async_computation.7 | async-start | bytes 5013504 | tf_op jit(solution)/shard_map/all_gather | solution.py:46
  220.9 335.2 %all-reduce.4.cloned.1.call-start = ((), (), s32[]{:S(2)}) async-start(), calls=%async_computation.4 | async-start | bytes 1179648 | tf_op jit(solution)/shard_map/psum | solution.py:69
  316.3 0.8 copy-start.4
  419.2 0.7 copy-start.6
  425.4 130.6 %copy-start.1 = (f32[128,384]{1,0:T(8,128)}, f32[128,384]{1,0:T(8,128)S(1)}, u32[]{:S(2)}) copy-start(f32[128,384]{1,0:T(8,128)S(1)} %fusion.76) | copy-start | bytes 589828
  428.7 278.9 %all-reduce.6.cloned.1.call-start = ((), (), s32[]{:S(2)}) async-start(), calls=%async_computation.5 | async-start | bytes 1179648 | tf_op jit(solution)/shard_map/psum | solution.py:69
  711.5 8.8 %copy-start.3 = (f32[128,384]{1,0:T(8,128)S(1)}, f32[128,384]{1,0:T(8,128)}, u32[]{:S(2)}) copy-start(f32[128,384]{1,0:T(8,128)} %param.6) | copy-start | bytes 589828
Sparse Core Ops, SparseCore 0:
  9.6 10.6 reduce-scatter.2
  23.1 80.8 all-gather.4
  214.2 6.6 reduce-scatter.4
  223.5 80.8 all-gather.6
  428.9 127.1 all-reduce.3
  578.9 128.7 all-reduce.5
